TPU v7x, 32 devices: a whole 2x2x4 slice. The times are simulated.
32 devices in a mesh: seq: 8 (over z, x), exp: 4 (over y, core).
Axes of the slice: x: 2, y: 2, z: 4, core: 2. Of those that a mesh axis runs over, the one named last changes fastest.
Arguments:
- tokens: bfloat16 [4, 1024, 4096], P('exp', 'seq'), may hold values from -6 to 6
- out_grad: bfloat16 [4, 1024, 4096], P('exp', 'seq'), may hold values from -0.59765625 to 0.59765625
- router_weight: bfloat16 [4096, 32], replicated, may hold values from -8 to 8
- gate_weight: bfloat16 [32, 4096, 768], P(('seq', 'exp')), may hold values from -0.09375 to 0.09375
- up_weight: bfloat16 [32, 4096, 768], P(('seq', 'exp')), may hold values from -0.09375 to 0.09375
- down_weight: bfloat16 [32, 768, 4096], P(('seq', 'exp')), may hold values from -0.21875 to 0.21875
- saved_gate: bfloat16 [32, 2048, 768], P(('seq', 'exp')), may hold values from -6 to 6
- saved_up: bfloat16 [32, 2048, 768], P(('seq', 'exp')), may hold values from -6 to 6
- expert_ids: int32 [4, 1024, 8], P('exp', 'seq'), may hold values from 0 to 31, as said below
- aux_weight: float32 [1], replicated, may hold values from 2 to 6
Outputs:
- token_grad: bfloat16 [4, 1024, 4096], P('exp', 'seq')
- combine_grad: float32 [4, 1024, 8], P('exp', 'seq')
- router_grad: float32 [4096, 32], P(('seq', 'exp'))
Inputs may be any that keep to these rules, and one draw needn't show every extreme that they name: `expert_ids`: among the rows of one device (128 tokens) each expert is named at most 64 times, and some expert exactly 64 times; a token's 8 experts differ.
All inputs are finite; a program needn't handle non-finite values.
Results may differ from a plain program's by a relative error of at most 0.013.
Values may be sent and summed in bfloat16 or wider, within the bound.
A program may use at most 192 MiB of HBM per device.

v0:
```python
import jax
import jax.numpy as jnp
from jax import lax
from jax.experimental import pallas as pl
from jax.experimental.pallas import tpu as pltpu
from jax.sharding import PartitionSpec as P


def expert_backward(grad_rows, gate_rows, w_gate, w_up, w_down, pre_gate, pre_up):
    upstream = jnp.einsum("rd,fd->rf", grad_rows, w_down, preferred_element_type=jnp.float32)
    first = pre_gate.astype(jnp.float32)
    second = pre_up.astype(jnp.float32)
    gate_sig = jax.nn.sigmoid(first)
    gate_act = first * gate_sig
    hidden = gate_act * second
    slot_combine = jnp.sum(upstream * hidden, axis=-1).astype(jnp.bfloat16)
    scaled = gate_rows.astype(jnp.float32)[:, None] * upstream
    grad_first = (scaled * second * gate_sig * (1.0 + first * (1.0 - gate_sig))).astype(
        jnp.bfloat16
    )
    grad_second = (scaled * gate_act).astype(jnp.bfloat16)
    back_rows = jnp.einsum("rf,df->rd", grad_first, w_gate, preferred_element_type=jnp.float32)
    back_rows = back_rows + jnp.einsum(
        "rf,df->rd", grad_second, w_up, preferred_element_type=jnp.float32
    )
    return (back_rows.astype(jnp.bfloat16), slot_combine)


def shards(
    tokens,
    out_grad,
    router_weight,
    gate_weight,
    up_weight,
    down_weight,
    saved_gate,
    saved_up,
    expert_ids,
    aux_weight,
):
    seq_size = lax.axis_size("seq")
    exp_size = lax.axis_size("exp")
    devices = seq_size * exp_size
    inputs = tokens[0]
    upstream_grad = out_grad[0]
    chosen_ids = expert_ids[0]
    tok_rows, top_count = chosen_ids.shape
    model_width = inputs.shape[1]
    experts = router_weight.shape[1]
    capacity = saved_gate.shape[1] // devices
    logits = jnp.dot(inputs, router_weight, preferred_element_type=jnp.float32)
    router_probs = jax.nn.softmax(logits, axis=-1)
    chosen = jnp.take_along_axis(router_probs, chosen_ids, axis=1)
    chosen_sum = jnp.sum(chosen, axis=1, keepdims=True)
    gate_vals = chosen / chosen_sum
    onehot = (
        chosen_ids.reshape(-1)[:, None] == jnp.arange(experts, dtype=jnp.int32)[None, :]
    ).astype(jnp.int32)
    rank_before = jnp.cumsum(onehot, axis=0) - onehot
    slot_pos = jnp.sum(rank_before * onehot, axis=1)
    slot_index = chosen_ids.reshape(-1) * capacity + slot_pos
    token_order = jnp.arange(tok_rows * top_count, dtype=jnp.int32) // top_count
    slot_token = (
        jnp.full((experts * capacity,), tok_rows, jnp.int32).at[slot_index].set(token_order)
    )
    grad_padded = jnp.concatenate(
        [upstream_grad, jnp.zeros((1, model_width), jnp.bfloat16)], axis=0
    )
    grad_slots = grad_padded[slot_token]
    gate_slots = (
        jnp.zeros((experts * capacity,), jnp.bfloat16)
        .at[slot_index]
        .set(gate_vals.reshape(-1).astype(jnp.bfloat16))
    )
    chosen_count = jnp.sum(onehot.reshape(tok_rows, top_count, experts), axis=1).astype(jnp.float32)
    local_counts = jnp.sum(chosen_count, axis=0)
    seq_counts = lax.psum(local_counts, "seq")
    recv_grad, recv_gate = (
        lax.all_to_all(
            grad_slots.reshape(experts, 1, capacity, model_width),
            ("seq", "exp"),
            split_axis=0,
            concat_axis=1,
            tiled=True,
        ),
        lax.all_to_all(
            gate_slots.reshape(experts, 1, capacity),
            ("seq", "exp"),
            split_axis=0,
            concat_axis=1,
            tiled=True,
        ),
    )
    back_rows, slot_combine = expert_backward(
        recv_grad.reshape(-1, model_width),
        recv_gate.reshape(-1),
        gate_weight[0],
        up_weight[0],
        down_weight[0],
        saved_gate[0],
        saved_up[0],
    )
    returned, combine_back = (
        lax.all_to_all(
            back_rows.reshape(1, devices, capacity, model_width),
            ("seq", "exp"),
            split_axis=1,
            concat_axis=0,
            tiled=True,
        ),
        lax.all_to_all(
            slot_combine.reshape(1, devices, capacity),
            ("seq", "exp"),
            split_axis=1,
            concat_axis=0,
            tiled=True,
        ),
    )
    returned_rows = returned.reshape(experts * capacity, model_width)
    expert_sum = jnp.sum(
        returned_rows[slot_index].reshape(tok_rows, top_count, model_width).astype(jnp.float32),
        axis=1,
    )
    combine_grad = (
        combine_back.reshape(-1)[slot_index].reshape(tok_rows, top_count).astype(jnp.float32)
    )
    prob_sel = (
        combine_grad - jnp.sum(gate_vals * combine_grad, axis=1, keepdims=True)
    ) / chosen_sum
    prob_grad = jnp.einsum(
        "tk,tke->te", prob_sel, onehot.reshape(tok_rows, top_count, experts).astype(jnp.float32)
    )
    fraction = experts * seq_counts / (top_count * tok_rows * seq_size)
    prob_grad = prob_grad + aux_weight[0] * fraction[None, :]
    dlogits = router_probs * (prob_grad - jnp.sum(router_probs * prob_grad, axis=1, keepdims=True))
    logit_grad = dlogits.astype(jnp.bfloat16)
    token_grad = expert_sum + jnp.einsum(
        "te,de->td", logit_grad, router_weight, preferred_element_type=jnp.float32
    )
    router_grad = lax.psum_scatter(
        jnp.einsum("td,te->de", inputs, logit_grad, preferred_element_type=jnp.float32),
        ("seq", "exp"),
        scatter_dimension=0,
        tiled=True,
    )
    return (token_grad.astype(jnp.bfloat16)[None], combine_grad[None], router_grad)

MESH = pl.DeviceIdType.MESH
CHUNK_ORDERS = (
    (False, False),
    (False, True),
    (True, False),
    (False, True),
    (False, False),
    (True, True),
    (False, True),
    (False, False),
)
CHUNKS = len(CHUNK_ORDERS)
LEVELS = 4
BLOCKS = 4 * LEVELS
STEP_WIDTH = 0.75


def place_of():
    seq, exp = lax.axis_index("seq"), lax.axis_index("exp")
    return seq // 2, seq % 2, exp // 2, exp % 2


def nearest(z, k):
    table = ((0, 1, 2, 3), (1, 2, 0, 3), (2, 1, 3, 0), (3, 2, 1, 0))
    value = jnp.int32(table[3][k])
    for level in (2, 1, 0):
        value = jnp.where(z == level, jnp.int32(table[level][k]), value)
    return value


def planar(first, second, swap):
    return (second, first) if swap else (first, second)


class Copies:
    def __init__(self, swap):
        self.z, self.x, self.y, self.c = place_of()
        self.swap = swap
        self.p, self.q = planar(self.x, self.y, swap)

    def block(self, z, p, q):
        x, y = planar(p, q, self.swap)
        return (z * 2 + x) * 2 + y

    def device(self, z, p, q):
        x, y = planar(p, q, self.swap)
        return z * 2 + x, y * 2 + self.c

    def remote(self, src, dst, send, recv, z, p, q):
        return pltpu.make_async_remote_copy(
            src_ref=src,
            dst_ref=dst,
            send_sem=send,
            recv_sem=recv,
            device_id=self.device(z, p, q),
            device_id_type=MESH,
        )


def sibling_copy(src, dst, send, recv):
    z, x, y, c = place_of()
    return pltpu.make_async_remote_copy(
        src_ref=src,
        dst_ref=dst,
        send_sem=send,
        recv_sem=recv,
        device_id=(z * 2 + x, y * 2 + 1 - c),
        device_id_type=MESH,
    )


def gather_names(chunk):
    if CHUNK_ORDERS[chunk][0]:
        middle = [("Z", k) for k in (1, 2, 3)] + [("P", k) for k in range(4)]
    else:
        middle = [("P", 0)] + [("Z", k) for k in (1, 2, 3)] + [("Y", k) for k in (1, 2, 3)]
    return [("own", 0)] + middle + [("Q", 0), ("near", 0), ("far", 0)]


def pipelined(names):
    timed = [
        (chunk + place * STEP_WIDTH, chunk, place, name)
        for chunk in range(CHUNKS)
        for place, name in enumerate(names(chunk))
    ]
    return [(chunk, name) for _, chunk, _, name in sorted(timed)]


def gather_kernel(
    grad_ref, place_ref, down_ref, up_ref, held, rows, down, own_sem, down_sem, send, recv, peer_send, peer_recv
):
    z, x, y, c = place_of()
    width = held.shape[-1]
    here = (z * 2 + x) * 2 + y
    started = []

    def start(copy, when=None):
        if when is None:
            copy.start()
        else:
            pl.when(when)(copy.start)
        started.append((copy, when))

    def own_copy(chunk):
        return pltpu.make_async_copy(
            grad_ref.at[:, pl.ds(chunk * width, width)], held.at[chunk, c, here], own_sem.at[chunk]
        )

    def down_copy(chunk):
        return pltpu.make_async_copy(
            down_ref.at[:, pl.ds(chunk * width, width)], down.at[chunk % 2], down_sem.at[chunk]
        )

    def multiply(chunk, core):
        @pl.loop(0, BLOCKS)
        def _(b):
            rows[b] = jnp.dot(
                place_ref[core, b], held[chunk, core, b], preferred_element_type=jnp.float32
            ).astype(jnp.bfloat16)

        group = 4

        @pl.loop(0, BLOCKS // group)
        def _(i):
            picked = rows[pl.ds(i * group, group)]
            term = lax.dot_general(
                picked.reshape(-1, width),
                down[chunk % 2],
                (((1,), (1,)), ((), ())),
                preferred_element_type=jnp.float32,
            ).reshape(group, -1, down.shape[1])
            if chunk == 0:
                up_ref[core, pl.ds(i * group, group)] = term
            else:
                up_ref[core, pl.ds(i * group, group)] += term

    def step(chunk, name):
        kind, k = name
        z_first, swap = CHUNK_ORDERS[chunk]
        near = Copies(swap)
        p, q = near.p, near.q

        def spread(block, index, dz=None, dp=0, dq=0, when=None):
            ref = held.at[chunk, c, block]
            start(
                near.remote(
                    ref,
                    ref,
                    send.at[chunk, index],
                    recv.at[chunk, block],
                    z if dz is None else z + dz,
                    1 - p if dp else p,
                    1 - q if dq else q,
                ),
                when,
            )

        def arrived(block):
            ref = held.at[chunk, c, block]
            near.remote(ref, ref, send.at[chunk, 0], recv.at[chunk, block], z, 1 - p, q).wait_recv()

        def both_ways(block, index):
            spread(block, index, dz=1, when=z < LEVELS - 1)
            spread(block, index + 1, dz=-1, when=z > 0)

        def onward(block, level, index):
            up = level < z
            spread(
                block,
                index,
                dz=jnp.where(up, 1, -1),
                when=jnp.where(up, z < LEVELS - 1, z > 0),
            )

        level = nearest(z, k)
        if kind == "own":
            own_copy(chunk).wait()
            block = near.block(z, p, q)
            if z_first:
                both_ways(block, 0)
                spread(block, 5, dp=1)
                spread(block, 9, dq=1)
            else:
                spread(block, 0, dp=1)
                both_ways(block, 1)
                spread(block, 11, dq=1)
        elif kind == "Z":
            block = near.block(level, p, q)
            arrived(block)
            if z_first:
                onward(block, level, 1 + k)
                spread(block, 5 + k, dp=1)
                spread(block, 9 + k, dq=1)
            else:
                onward(block, level, 2 + k)
                spread(block, 11 + k, dq=1)
        elif kind == "P":
            block = near.block(level, 1 - p, q)
            arrived(block)
            if z_first:
                spread(block, 13 + k, dq=1)
            else:
                both_ways(block, 6)
                spread(block, 15, dq=1)
        elif kind == "Y":
            block = near.block(level, 1 - p, q)
            arrived(block)
            onward(block, level, 7 + k)
            spread(block, 15 + k, dq=1)
        elif kind == "Q":
            for other in range(LEVELS):
                for side in range(2):
                    arrived(near.block(other, side, 1 - q))
            ref = held.at[chunk, c]
            start(sibling_copy(ref, ref, peer_send.at[chunk], peer_recv.at[chunk]))
        elif kind == "near":
            down_copy(chunk).wait()
            multiply(chunk, c)
        elif kind == "far":
            ref = held.at[chunk, 1 - c]
            sibling_copy(ref, ref, peer_send.at[chunk], peer_recv.at[chunk]).wait_recv()
            multiply(chunk, 1 - c)
            if chunk + 2 < CHUNKS:
                down_copy(chunk + 2).start()

    for chunk in range(CHUNKS):
        own_copy(chunk).start()
    down_copy(0).start()
    down_copy(1).start()
    for chunk, name in pipelined(gather_names):
        step(chunk, name)
    for copy, when in started:
        if when is None:
            copy.wait_send()
        else:
            pl.when(when)(copy.wait_send)


def gather_call(grad, place, down_weight):
    rows, model_width = grad.shape
    hidden = down_weight.shape[0]
    capacity = place.shape[2]
    width = model_width // CHUNKS
    dma = pltpu.SemaphoreType.DMA
    return pl.pallas_call(
        gather_kernel,
        out_shape=jax.ShapeDtypeStruct((2, BLOCKS, capacity, hidden), jnp.float32),
        in_specs=[
            pl.BlockSpec(memory_space=pl.ANY),
            pl.BlockSpec(memory_space=pltpu.VMEM),
            pl.BlockSpec(memory_space=pl.ANY),
        ],
        out_specs=pl.BlockSpec(memory_space=pltpu.VMEM),
        scratch_shapes=[
            pltpu.VMEM((CHUNKS, 2, BLOCKS, rows, width), jnp.bfloat16),
            pltpu.VMEM((BLOCKS, capacity, width), jnp.bfloat16),
            pltpu.VMEM((2, hidden, width), jnp.bfloat16),
            dma((CHUNKS,)),
            dma((CHUNKS,)),
            dma((CHUNKS, 19)),
            dma((CHUNKS, BLOCKS)),
            dma((CHUNKS,)),
            dma((CHUNKS,)),
        ],
        compiler_params=pltpu.CompilerParams(
            has_side_effects=True, vmem_limit_bytes=60 * 2**20
        ),
        name="gather_upstream",
    )(grad, place, down_weight)


def return_names(chunk):
    if CHUNK_ORDERS[chunk][0]:
        middle = [("P", k) for k in (3, 2, 1, 0)] + [("Z", k) for k in (3, 2, 1)]
    else:
        middle = [("Y", k) for k in (3, 2, 1)] + [("Z", k) for k in (3, 2, 1)] + [("P", 0)]
    return [("away", 0), ("near", 0)] + middle + [("own", 0)]


def return_kernel(
    first_ref,
    second_ref,
    join_ref,
    gate_ref,
    up_ref,
    out_ref,
    held,
    landed,
    leaving,
    weights,
    weight_sem,
    send,
    recv,
    peer_send,
    peer_recv,
):
    z, x, y, c = place_of()
    capacity = first_ref.shape[2]
    width = held.shape[-1]
    hidden = first_ref.shape[3]
    started = []

    def start(copy, when=None):
        if when is None:
            copy.start()
        else:
            pl.when(when)(copy.start)
        started.append((copy, when))

    def weight_copies(chunk):
        return [
            pltpu.make_async_copy(
                ref.at[pl.ds(chunk * width, width)],
                weights.at[chunk % 2, i],
                weight_sem.at[chunk, i],
            )
            for i, ref in enumerate((gate_ref, up_ref))
        ]

    def back_rows(chunk, core, store):
        group = 4

        @pl.loop(0, BLOCKS // group)
        def _(i):
            total = None
            for j, ref in enumerate((first_ref, second_ref)):
                term = lax.dot_general(
                    ref[core, pl.ds(i * group, group)].reshape(-1, hidden),
                    weights[chunk % 2, j],
                    (((1,), (1,)), ((), ())),
                    preferred_element_type=jnp.float32,
                )
                total = term if total is None else total + term
            store(i * group, group, total.astype(jnp.bfloat16).reshape(group, capacity, width))

    def leave(chunk):
        return sibling_copy(
            leaving.at[chunk % 2],
            held.at[chunk, :, pl.ds(capacity, capacity)],
            peer_send.at[chunk],
            peer_recv.at[chunk],
        )

    def step(chunk, name):
        kind, k = name
        z_first, swap = CHUNK_ORDERS[chunk]
        near = Copies(swap)
        p, q = near.p, near.q

        def give(block, slot, index, dz=None, dp=0, dq=0, when=None):
            start(
                near.remote(
                    held.at[chunk, block],
                    landed.at[chunk, slot],
                    send.at[chunk, index],
                    recv.at[chunk, slot],
                    z if dz is None else z + dz,
                    1 - p if dp else p,
                    1 - q if dq else q,
                ),
                when,
            )

        def take(block, slot):
            ref = landed.at[chunk, slot]
            near.remote(ref, ref, send.at[chunk, 0], recv.at[chunk, slot], z, 1 - p, q).wait_recv()
            held[chunk, block] = (
                held[chunk, block].astype(jnp.float32) + landed[chunk, slot].astype(jnp.float32)
            ).astype(jnp.bfloat16)

        def take_outer(block, level, base):
            pl.when(jnp.where(level > z, z > 0, z < LEVELS - 1))(lambda: take(block, base + level))

        def give_inner(block, level, base, index):
            up = level > z
            last = level == z - 1
            give(
                block,
                base + jnp.where(last, LEVELS, level),
                index,
                dz=jnp.where(up, 1, -1),
            )

        def take_ends(block, base):
            pl.when(z > 0)(lambda: take(block, base + z))
            pl.when(z < LEVELS - 1)(lambda: take(block, base + LEVELS))

        level = nearest(z, k)
        if kind == "away":
            for copy in weight_copies(chunk):
                copy.wait()
            if chunk >= 2:
                leave(chunk - 2).wait_send()

            def store(at, count, value):
                leaving[chunk % 2, pl.ds(at, count)] = value

            back_rows(chunk, 1 - c, store)
            leave(chunk).start()
        elif kind == "near":

            def store(at, count, value):
                held[chunk, pl.ds(at, count), pl.ds(0, capacity)] = value

            back_rows(chunk, c, store)
            if chunk + 2 < CHUNKS:
                for copy in weight_copies(chunk + 2):
                    copy.start()
            leave(chunk).wait_recv()

            @pl.loop(0, BLOCKS)
            def _(b):
                held[chunk, b] = jnp.dot(
                    join_ref[b], held[chunk, b], preferred_element_type=jnp.float32
                ).astype(jnp.bfloat16)

            for side in (1, 0):
                for far in (3, 2, 1, 0):
                    other = nearest(z, far)
                    column = 1 - p if side else p
                    give(
                        near.block(other, column, 1 - q),
                        other * 2 + column,
                        far * 2 + side,
                        dq=1,
                    )
        elif kind == "P" and z_first:
            block = near.block(level, 1 - p, q)
            take(block, level * 2 + 1 - p)
            give(block, 8 + level, 8 + k, dp=1)
        elif kind == "P":
            block = near.block(z, 1 - p, q)
            take(block, z * 2 + 1 - p)
            take_ends(block, 13)
            give(block, 18, 14, dp=1)
        elif kind == "Z":
            block = near.block(level, p, q)
            take(block, level * 2 + p)
            if z_first:
                take(block, 8 + level)
                take_outer(block, level, 12)
                give_inner(block, level, 12, 11 + k)
            else:
                take_outer(block, level, 8)
                give_inner(block, level, 8, 7 + k)
        elif kind == "Y":
            block = near.block(level, 1 - p, q)
            take(block, level * 2 + 1 - p)
            take_outer(block, level, 13)
            give_inner(block, level, 13, 10 + k)
        elif kind == "own":
            block = near.block(z, p, q)
            take(block, z * 2 + p)
            if z_first:
                take(block, 8 + z)
                take_ends(block, 12)
            else:
                take_ends(block, 8)
                take(block, 18)
            out_ref[:, chunk * width : (chunk + 1) * width] = held[chunk, block]

    for chunk in range(2):
        for copy in weight_copies(chunk):
            copy.start()
    for chunk, name in pipelined(return_names):
        step(chunk, name)
    for chunk in range(CHUNKS - 2, CHUNKS):
        leave(chunk).wait_send()
    for copy, when in started:
        if when is None:
            copy.wait_send()
        else:
            pl.when(when)(copy.wait_send)


def return_call(first, second, joined, gate_weight, up_weight):
    model_width, hidden = gate_weight.shape
    capacity = first.shape[2]
    rows = joined.shape[1]
    width = model_width // CHUNKS
    dma = pltpu.SemaphoreType.DMA
    vmem, anywhere = pl.BlockSpec(memory_space=pltpu.VMEM), pl.BlockSpec(memory_space=pl.ANY)
    return pl.pallas_call(
        return_kernel,
        out_shape=jax.ShapeDtypeStruct((rows, model_width), jnp.bfloat16),
        in_specs=[vmem, vmem, vmem, anywhere, anywhere],
        out_specs=vmem,
        scratch_shapes=[
            pltpu.VMEM((CHUNKS, BLOCKS, rows, width), jnp.bfloat16),
            pltpu.VMEM((CHUNKS, 19, rows, width), jnp.bfloat16),
            pltpu.VMEM((2, BLOCKS, capacity, width), jnp.bfloat16),
            pltpu.VMEM((2, 2, width, hidden), jnp.bfloat16),
            dma((CHUNKS, 2)),
            dma((CHUNKS, 15)),
            dma((CHUNKS, 19)),
            dma((CHUNKS,)),
            dma((CHUNKS,)),
        ],
        compiler_params=pltpu.CompilerParams(
            has_side_effects=True, vmem_limit_bytes=60 * 2**20
        ),
        name="back_return",
    )(first, second, joined, gate_weight, up_weight)


def silu_terms(pre_gate, pre_up):
    first = pre_gate.astype(jnp.float32)
    second = pre_up.astype(jnp.float32)
    gate_sig = jax.nn.sigmoid(first)
    gate_act = first * gate_sig
    return second * gate_sig * (1.0 + first * (1.0 - gate_sig)), gate_act, gate_act * second


def gathered_shards(
    tokens,
    out_grad,
    router_weight,
    gate_weight,
    up_weight,
    down_weight,
    saved_gate,
    saved_up,
    expert_ids,
    aux_weight,
):
    both = ("seq", "exp")
    seq_size = lax.axis_size("seq")
    exp_size = lax.axis_size("exp")
    devices = seq_size * exp_size
    inputs = tokens[0]
    chosen_ids = expert_ids[0]
    tok_rows, top_count = chosen_ids.shape
    model_width = inputs.shape[1]
    experts = router_weight.shape[1]
    capacity = saved_gate.shape[1] // devices

    logits = jnp.dot(inputs, router_weight, preferred_element_type=jnp.float32)
    router_probs = jax.nn.softmax(logits, axis=-1)
    onehot = (chosen_ids[:, :, None] == jnp.arange(experts, dtype=jnp.int32)).astype(jnp.float32)
    picked = jnp.sum(onehot, axis=1)
    chosen_sum = jnp.sum(router_probs * picked, axis=1, keepdims=True)
    gate_dense = router_probs * picked / chosen_sum
    earlier = jnp.tril(jnp.ones((tok_rows, tok_rows), jnp.bfloat16), -1)
    rank = jnp.dot(earlier, picked.astype(jnp.bfloat16), preferred_element_type=jnp.float32)
    slot_pos = jnp.where(picked > 0, rank, -1.0)
    sent = jnp.stack([slot_pos.T, gate_dense.astype(jnp.bfloat16).astype(jnp.float32).T], axis=1)
    received = lax.all_to_all(sent, both, split_axis=0, concat_axis=0, tiled=True)

    counts = jnp.sum((received[:, 0] >= 0).astype(jnp.float32), axis=1)
    counts = jnp.tile(jnp.sum(counts.reshape(seq_size, exp_size), axis=0), seq_size)

    def by_core(value):
        return jnp.swapaxes(value.reshape((devices // 2, 2) + value.shape[1:]), 0, 1)

    here_core = lax.axis_index("exp") % 2
    pos = received[:, 0].astype(jnp.int32)
    slot_ids = jnp.arange(capacity, dtype=jnp.int32)[None, :, None]
    at_slot = pos[:, None, :] == slot_ids
    gate_rows = jnp.sum(jnp.where(at_slot, received[:, 1][:, None, :], 0.0), axis=2)[:, :, None]
    place = by_core(at_slot.astype(jnp.bfloat16))
    pos_by_core = by_core(received[:, 0])
    own_pos = lax.dynamic_index_in_dim(pos_by_core, here_core, 0, keepdims=False)
    sent_pos = lax.dynamic_index_in_dim(pos_by_core, 1 - here_core, 0, keepdims=False)
    other_pos = lax.ppermute(sent_pos, "exp", [(i, i ^ 1) for i in range(exp_size)])
    join_pos = jnp.concatenate(
        [
            jnp.broadcast_to(own_pos[:, :, None], (devices // 2, tok_rows, capacity)),
            jnp.broadcast_to(other_pos[:, :, None], (devices // 2, tok_rows, capacity)),
        ],
        axis=2,
    ).astype(jnp.int32)
    joined = (join_pos == jnp.arange(2 * capacity, dtype=jnp.int32) % capacity).astype(jnp.bfloat16)

    upstream = gather_call(out_grad[0], place, down_weight[0])

    hidden_width = saved_gate.shape[2]
    blocks = (devices, capacity, hidden_width)
    slope, gate_act, hidden = silu_terms(
        by_core(saved_gate[0].reshape(blocks)), by_core(saved_up[0].reshape(blocks))
    )
    slot_combine = jnp.sum(upstream * hidden, axis=-1).astype(jnp.bfloat16)
    scaled = by_core(gate_rows) * upstream
    grad_first = (scaled * slope).astype(jnp.bfloat16)
    grad_second = (scaled * gate_act).astype(jnp.bfloat16)

    slot_combine = jnp.swapaxes(slot_combine, 0, 1).reshape(devices, capacity)
    combine_tok = jnp.sum(
        jnp.where(at_slot, slot_combine.astype(jnp.float32)[:, :, None], 0.0), axis=1
    )
    reply = jnp.stack([combine_tok, jnp.broadcast_to(counts[:, None], combine_tok.shape)], axis=1)
    answered = lax.all_to_all(reply, both, split_axis=0, concat_axis=0, tiled=True)

    expert_sum = return_call(grad_first, grad_second, joined, gate_weight[0], up_weight[0])

    combine_dense = answered[:, 0].T
    seq_counts = answered[:, 1, 0]
    combine_grad = jnp.sum(onehot * combine_dense[:, None, :], axis=2)
    mixed = jnp.sum(gate_dense * combine_dense, axis=1, keepdims=True)
    prob_grad = picked * (combine_dense - mixed) / chosen_sum
    fraction = experts * seq_counts / (top_count * tok_rows * seq_size)
    prob_grad = prob_grad + aux_weight[0] * fraction[None, :]
    dlogits = router_probs * (prob_grad - jnp.sum(router_probs * prob_grad, axis=1, keepdims=True))
    logit_grad = dlogits.astype(jnp.bfloat16)

    router_terms = jnp.einsum("te,td->ed", logit_grad, inputs, preferred_element_type=jnp.float32)
    router_terms = router_terms.reshape(experts, devices, model_width // devices)
    router_terms = lax.all_to_all(
        router_terms.transpose(1, 0, 2), both, split_axis=0, concat_axis=0, tiled=True
    )
    router_grad = jnp.sum(router_terms, axis=0).T

    token_grad = expert_sum.astype(jnp.float32) + jnp.einsum(
        "te,de->td", logit_grad, router_weight, preferred_element_type=jnp.float32
    )
    return (token_grad.astype(jnp.bfloat16)[None], combine_grad[None], router_grad)


def program(*arrays):
    tok_rows = arrays[0].shape[1]
    seq_size, exp_size = lax.axis_size("seq"), lax.axis_size("exp")
    slots = arrays[6].shape[1]
    lined = exp_size == 4 and seq_size == 2 * LEVELS
    fits = arrays[0].shape[2] == 4096 and arrays[6].shape[2] == 768 and tok_rows == 128
    if lined and fits and seq_size * exp_size * tok_rows <= 2 * slots:
        return gathered_shards(*arrays)
    return shards(*arrays)


def solution(mesh):
    placed = (
        P("exp", "seq", None),
        P("exp", "seq", None),
        P(),
        P(("seq", "exp"), None, None),
        P(("seq", "exp"), None, None),
        P(("seq", "exp"), None, None),
        P(("seq", "exp"), None, None),
        P(("seq", "exp"), None, None),
        P("exp", "seq", None),
        P(),
    )
    return jax.shard_map(
        program,
        mesh=mesh,
        in_specs=placed,
        out_specs=(P("exp", "seq", None), P("exp", "seq", None), P(("seq", "exp"), None)),
        check_vma=False,
    )
```

profile of v0, /device:TPU:8, one launch (start us, length us, event | category | flops | bytes accessed | tf_op | source)
XLA Modules:
  0.0 418.3 jit_solution(12873414872561453033)
XLA Ops:
  0.6 0.0 copy-start
  0.7 0.7 convert_reduce_fusion
  1.4 0.2 copy-done
  1.6 1.7 fusion.34
  3.3 0.0 copy-start.3
  3.3 0.0 copy-start.5
  3.4 0.0 copy-start.4
  3.4 0.2 fusion.11
  3.6 0.3 copy-done.3
  3.9 0.0 copy-done.5
  3.9 0.0 copy-done.4
  3.9 0.6 copy.43
  4.6 6.0 %all-to-all-start = ((f32[32,2,128]{2,1,0:T(2,128)}), f32[32,2,128]{2,1,0:T(2,128)S(1)}, u32[]{:S(2)}, u32[]{:S(2)}) async-start(f32[32,2,128]{2,1,0:T(2,128)} %copy.43), calls=%async_computation | async-start | bytes 65536 | tf_op jit(solution)/shard_map/all_to_all | solution.py:694
  11.3 2.3 copy.52
  13.5 0.5 and_select_fusion
  14.0 2.6 all-to-all-done
  16.7 0.3 fusion.33
  17.0 0.1 reshape.67
  17.1 0.1 broadcast_in_dim_tile.3
  17.2 1.0 fusion.16.place_ref
  18.1 0.0 copy-start.1
  18.1 153.2 %gather_upstream.1 = f32[2,16,64,768]{3,2,1,0:T(8,128)} custom-call(bf16[128,4096]{1,0:T(8,128)(2,1)} %bitcast.106, bf16[2,16,64,128]{3,2,1,0:T(8,128)(2,1)} %fusion.16.place_ref, bf16[768,4096]{1,0:T(8,128)(2,1)} %bitcast.101), custom_call_target="tpu_custom_call" | custom-call | tf_op jit(solution)/shard_map/gather_upstream/pallas_call | solution.py:392
  171.3 0.0 copy-done.1
  171.3 4.9 %fusion.8 = bf16[2,16,64]{2,1,0:T(8,128)(2,1)S(1)} fusion(f32[2,16,64,768]{3,2,1,0:T(8,128)} %gather_upstream.1, bf16[16,2,64,768]{3,2,1,0:T(8,128)(2,1)S(1)} %bitcast.97, bf16[16,2,64,768]{3,2,1,0:T(8,128)(2,1)} %bitcast.99), kind=kLoop, calls=%fused_computation.13 | loop fusion | flops 14153728 | bytes 12587008 | tf_op jit(solution)/shard_map/reduce_sum | solution.py:728
  176.2 0.7 select_reduce_fusion.1
  176.9 0.1 stack_broadcast_in_dim.2
  177.0 0.6 copy.49
  177.7 15.5 %all-to-all-start.1 = ((f32[32,2,128]{2,1,0:T(2,128)}), f32[32,2,128]{2,1,0:T(2,128)S(1)}, u32[]{:S(2)}, u32[]{:S(2)}) async-start(f32[32,2,128]{2,1,0:T(2,128)} %copy.49), calls=%async_computation.1 | async-start | bytes 65536 | tf_op jit(solution)/shard_map/all_to_all | solution.py:738
  193.2 0.6 constant_dynamic-slice_fusion.1
  193.8 0.1 collective-permute-start
  193.9 5.3 %all-to-all-done.1 = f32[32,2,128]{2,1,0:T(2,128)S(1)} async-done(((f32[32,2,128]{2,1,0:T(2,128)}), f32[32,2,128]{2,1,0:T(2,128)S(1)}, u32[]{:S(2)}, u32[]{:S(2)}) %all-to-all-start.1) | async-done | bytes 32800 | tf_op jit(solution)/shard_map/all_to_all | solution.py:738
  199.2 0.6 multiply_reduce_fusion.1
  199.9 0.3 fusion.23
  200.2 0.8 multiply_reduce_fusion
  201.0 0.8 multiply_convert_fusion.1
  201.7 2.5 convolution_bitcast_fusion
  204.2 4.4 %all-to-all-start.2 = ((f32[32,32,128]{2,1,0:T(8,128)}), f32[32,32,128]{2,1,0:T(8,128)}, u32[]{:S(2)}, u32[]{:S(2)}) async-start(f32[32,32,128]{2,1,0:T(8,128)} %convolution_bitcast_fusion), calls=%async_computation.2 | async-start | bytes 1048576 | tf_op jit(solution)/shard_map/all_to_all | solution.py:754
  208.6 0.0 copy-start.6
  208.6 7.3 %multiply_convert_fusion = (bf16[2,16,64,768]{3,2,1,0:T(8,128)(2,1)}, bf16[2,16,64,768]{3,2,1,0:T(8,128)(2,1)}) fusion(f32[2,16,64,768]{3,2,1,0:T(8,128)} %gather_upstream.1, f32[2,16,64]{2,1,0:T(8,128)S(1)} %copy.44, bf16[16,2,64,768]{3,2,1,0:T(8,128)(2,1)S(1)} %bitcast.98, bf16[16,2,64,768]{3,2,1,0:T(8,128)(2,1)} %bitcast.100), kind=kLoop, calls=%fused_computation.14 | loop fusion | flops 25165824 | bytes 18882560 | tf_op jit(solution)/shard_map/convert_element_type | solution.py:731
  216.0 0.0 collective-permute-done
  216.0 0.3 broadcast_in_dim.75
  216.3 0.3 broadcast_in_dim.74
  216.6 0.0 copy-done.6
  216.6 1.2 fusion.15.join_ref
  217.8 0.0 copy-start.2
  217.8 195.5 %back_return.1 = bf16[128,4096]{1,0:T(8,128)(2,1)} custom-call(bf16[2,16,64,768]{3,2,1,0:T(8,128)(2,1)} %get-tuple-element.8.first_ref, bf16[2,16,64,768]{3,2,1,0:T(8,128)(2,1)} %get-tuple-element.7.second_ref, bf16[16,128,128]{2,1,0:T(8,128)(2,1)} %fusion.15.join_ref, bf16[4096,768]{1,0:T(8,128)(2,1)} %bitcast.102, bf16[4096,768]{1,0:T(8,128)(2,1)} %bitcast.103), custom_call_target="tpu_custom_call" | custom-call | tf_op jit(solution)/shard_map/back_return/pallas_call | solution.py:630
  413.3 0.0 copy-done.2
  413.3 0.6 select_reduce_fusion.2
  413.9 2.7 fusion.10
  416.6 0.0 all-to-all-done.2
  416.6 1.7 reduce_sum.119
  (13 shorter events, 0.1 us)
Async XLA Ops:
  0.6 1.0 copy-start
  3.3 0.6 copy-start.3
  3.3 0.6 copy-start.5
  3.4 0.5 copy-start.4
  4.6 12.1 %all-to-all-start = ((f32[32,2,128]{2,1,0:T(2,128)}), f32[32,2,128]{2,1,0:T(2,128)S(1)}, u32[]{:S(2)}, u32[]{:S(2)}) async-start(f32[32,2,128]{2,1,0:T(2,128)} %copy.43), calls=%async_computation | async-start | bytes 65536 | tf_op jit(solution)/shard_map/all_to_all | solution.py:694
  18.1 153.2 %copy-start.1 = (bf16[1,2048,768]{2,1,0:T(8,128)(2,1)S(1)}, bf16[1,2048,768]{2,1,0:T(8,128)(2,1)}, u32[]{:S(2)}) copy-start(bf16[1,2048,768]{2,1,0:T(8,128)(2,1)} %param.16) | copy-start | bytes 9437188
  177.7 21.6 %all-to-all-start.1 = ((f32[32,2,128]{2,1,0:T(2,128)}), f32[32,2,128]{2,1,0:T(2,128)S(1)}, u32[]{:S(2)}, u32[]{:S(2)}) async-start(f32[32,2,128]{2,1,0:T(2,128)} %copy.49), calls=%async_computation.1 | async-start | bytes 65536 | tf_op jit(solution)/shard_map/all_to_all | solution.py:738
  193.8 22.2 %collective-permute-start = (f32[16,128]{1,0:T(8,128)}, f32[16,128]{1,0:T(8,128)S(1)}, u32[]{:S(2)}, u32[]{:S(2)}) collective-permute-start(f32[16,128]{1,0:T(8,128)} %bitcast.21), channel_id=1, source_target_pairs={{0,1},{1,0},{2,3},{3,2},{4,5},{5,4},{6,7},{7,6},{8,9},{9,8},{10,11... | collective-permute-start | bytes 24584 | tf_op jit(solution)/shard_map/ppermute | solution.py:711
  204.2 212.4 %all-to-all-start.2 = ((f32[32,32,128]{2,1,0:T(8,128)}), f32[32,32,128]{2,1,0:T(8,128)}, u32[]{:S(2)}, u32[]{:S(2)}) async-start(f32[32,32,128]{2,1,0:T(8,128)} %convolution_bitcast_fusion), calls=%async_computation.2 | async-start | bytes 1048576 | tf_op jit(solution)/shard_map/all_to_all | solution.py:754
  208.6 8.0 %copy-start.6 = (s32[128]{0:T(128)S(1)}, s32[128]{0:T(128)}, u32[]{:S(2)}) copy-start(s32[128]{0:T(128)} %and_select_fusion) | copy-start | bytes 1540
  217.8 195.5 %copy-start.2 = (s32[1,128,8]{1,2,0:T(8,128)S(1)}, s32[1,128,8]{1,2,0:T(8,128)}, u32[]{:S(2)}) copy-start(s32[1,128,8]{1,2,0:T(8,128)} %param.18) | copy-start | bytes 12292
where the time goes:
time: 419 us; the launch traced here: 418 us
  Pallas kernels  349 us (83%)
  starting transfers between devices  26 us (6%)
  other arithmetic  21.5 us (5%)
  waiting for transfers between devices  7.93 us (2%)
  matrix products  7.09 us (2%)
  local copies, waits for them, and re-layouts  5.6 us (1%)
    pallas_call x1, Pallas kernels, return_call(): pl.pallas_call(return_kernel, out_shape=jax.ShapeDtypeStruct((rows, model...  196 us
    pallas_call x1, Pallas kernels, gather_call(): pl.pallas_call(gather_kernel, out_shape=jax.ShapeDtypeStruct((2, BLOCKS,...  153 us
    all_to_all x1, starting transfers between devices, gathered_shards(): lax.all_to_all(reply, both, split_axis=0, concat_axis=0, tiled=True)  15.5 us
  transfers between devices with their start and end apart: 4, of which 2 were waited for; matrix products, arithmetic and copies ran while one was open for 5% of the time, Pallas kernels for 47%

commit v1 on v0

--- a/solution.py
+++ b/solution.py
@@ -146,20 +146,27 @@
     return (token_grad.astype(jnp.bfloat16)[None], combine_grad[None], router_grad)
 
 MESH = pl.DeviceIdType.MESH
-CHUNK_ORDERS = (
-    (False, False),
-    (False, True),
-    (True, False),
-    (False, True),
-    (False, False),
-    (True, True),
-    (False, True),
-    (False, False),
+GATHER_TYPES = ((False, False), (False, True), (True, False), (False, True), (False, False), (True, True), (False, True), (False, False))
+RETURN_TYPES = ((False, False), (False, True), (False, False), (False, True), (True, True), (True, False), (False, True), (False, False))
+GATHER_ORDER = (
+    60, 40, 80, 100, 20, 0, 101, 42, 41, 120, 22, 44, 21, 2, 102, 1, 23, 121, 140, 61, 43, 3, 24, 6,
+    7, 5, 26, 25, 45, 81, 106, 62, 47, 4, 63, 103, 46, 65, 27, 85, 104, 8, 66, 142, 9, 86, 107, 83,
+    82, 10, 28, 122, 64, 29, 84, 67, 125, 123, 105, 143, 48, 30, 87, 68, 141, 49, 69, 126, 50, 124,
+    145, 88, 70, 89, 108, 146, 127, 109, 144, 90, 128, 147, 110, 129, 148, 149, 130, 150,
 )
-CHUNKS = len(CHUNK_ORDERS)
+RETURN_ORDER = (
+    0, 20, 1, 2, 3, 21, 22, 10, 27, 4, 26, 40, 6, 11, 23, 8, 28, 60, 12, 30, 41, 42, 13, 61, 67, 62,
+    46, 33, 80, 50, 47, 100, 43, 45, 7, 5, 53, 24, 81, 31, 63, 120, 51, 82, 64, 34, 101, 140, 68,
+    103, 48, 32, 85, 83, 54, 106, 107, 44, 70, 66, 121, 141, 105, 55, 146, 35, 108, 90, 124, 123,
+    122, 14, 93, 73, 144, 128, 25, 84, 15, 130, 126, 102, 109, 86, 142, 74, 125, 127, 143, 36, 132,
+    104, 72, 129, 65, 71, 9, 92, 29, 153, 110, 131, 52, 145, 113, 150, 56, 16, 151, 49, 111, 133,
+    75, 112, 94, 88, 114, 76, 152, 87, 148, 91, 147, 57, 115, 136, 89, 149, 134, 69, 135, 37, 116,
+    95, 156, 154, 96, 155, 117, 137, 17, 97, 77, 157,
+)
+
+CHUNKS = len(GATHER_TYPES)
 LEVELS = 4
 BLOCKS = 4 * LEVELS
-STEP_WIDTH = 0.75
 
 
 def place_of():
@@ -217,20 +224,15 @@
 
 
 def gather_names(chunk):
-    if CHUNK_ORDERS[chunk][0]:
+    if GATHER_TYPES[chunk][0]:
         middle = [("Z", k) for k in (1, 2, 3)] + [("P", k) for k in range(4)]
     else:
         middle = [("P", 0)] + [("Z", k) for k in (1, 2, 3)] + [("Y", k) for k in (1, 2, 3)]
     return [("own", 0)] + middle + [("Q", 0), ("near", 0), ("far", 0)]
 
 
-def pipelined(names):
-    timed = [
-        (chunk + place * STEP_WIDTH, chunk, place, name)
-        for chunk in range(CHUNKS)
-        for place, name in enumerate(names(chunk))
-    ]
-    return [(chunk, name) for _, chunk, _, name in sorted(timed)]
+def listed(order, names):
+    return [(code // 20, names(code // 20)[code % 20]) for code in order]
 
 
 def gather_kernel(
@@ -259,7 +261,7 @@
         )
 
     def multiply(chunk, core):
-        @pl.loop(0, BLOCKS)
+        @pl.loop(0, BLOCKS, unroll=4)
         def _(b):
             rows[b] = jnp.dot(
                 place_ref[core, b], held[chunk, core, b], preferred_element_type=jnp.float32
@@ -283,7 +285,7 @@
 
     def step(chunk, name):
         kind, k = name
-        z_first, swap = CHUNK_ORDERS[chunk]
+        z_first, swap = GATHER_TYPES[chunk]
         near = Copies(swap)
         p, q = near.p, near.q
 
@@ -374,7 +376,7 @@
         own_copy(chunk).start()
     down_copy(0).start()
     down_copy(1).start()
-    for chunk, name in pipelined(gather_names):
+    for chunk, name in listed(GATHER_ORDER, gather_names):
         step(chunk, name)
     for copy, when in started:
         if when is None:
@@ -417,11 +419,12 @@
 
 
 def return_names(chunk):
-    if CHUNK_ORDERS[chunk][0]:
+    if RETURN_TYPES[chunk][0]:
         middle = [("P", k) for k in (3, 2, 1, 0)] + [("Z", k) for k in (3, 2, 1)]
     else:
         middle = [("Y", k) for k in (3, 2, 1)] + [("Z", k) for k in (3, 2, 1)] + [("P", 0)]
-    return [("away", 0), ("near", 0)] + middle + [("own", 0)]
+    leaves = [("leaf", (side, k)) for side in (1, 0) for k in (3, 2, 1, 0)]
+    return [("away", 0), ("near", 0)] + leaves + middle + [("own", 0)]
 
 
 def return_kernel(
@@ -490,7 +493,7 @@
 
     def step(chunk, name):
         kind, k = name
-        z_first, swap = CHUNK_ORDERS[chunk]
+        z_first, swap = RETURN_TYPES[chunk]
         near = Copies(swap)
         p, q = near.p, near.q
 
@@ -532,7 +535,7 @@
             pl.when(z > 0)(lambda: take(block, base + z))
             pl.when(z < LEVELS - 1)(lambda: take(block, base + LEVELS))
 
-        level = nearest(z, k)
+        level = None if kind == "leaf" else nearest(z, k)
         if kind == "away":
             for copy in weight_copies(chunk):
                 copy.wait()
@@ -555,22 +558,16 @@
                     copy.start()
             leave(chunk).wait_recv()
 
-            @pl.loop(0, BLOCKS)
+            @pl.loop(0, BLOCKS, unroll=4)
             def _(b):
                 held[chunk, b] = jnp.dot(
                     join_ref[b], held[chunk, b], preferred_element_type=jnp.float32
                 ).astype(jnp.bfloat16)
-
-            for side in (1, 0):
-                for far in (3, 2, 1, 0):
-                    other = nearest(z, far)
-                    column = 1 - p if side else p
-                    give(
-                        near.block(other, column, 1 - q),
-                        other * 2 + column,
-                        far * 2 + side,
-                        dq=1,
-                    )
+        elif kind == "leaf":
+            side, far = k
+            level = nearest(z, far)
+            column = 1 - p if side else p
+            give(near.block(level, column, 1 - q), level * 2 + column, far * 2 + side, dq=1)
         elif kind == "P" and z_first:
             block = near.block(level, 1 - p, q)
             take(block, level * 2 + 1 - p)
@@ -609,7 +606,7 @@
     for chunk in range(2):
         for copy in weight_copies(chunk):
             copy.start()
-    for chunk, name in pipelined(return_names):
+    for chunk, name in listed(RETURN_ORDER, return_names):
         step(chunk, name)
     for chunk in range(CHUNKS - 2, CHUNKS):
         leave(chunk).wait_send()

time: 419 us -> 353 us (0.84)
  Pallas kernels: 349 us -> 285 us
    pallas_call x1, Pallas kernels: 196 us -> 148 us  [return_call(): pl.pallas_call(return_kernel, out_shape=jax.ShapeDtypeStruct((rows, model...]
    pallas_call x1, Pallas kernels: 153 us -> 137 us  [gather_call(): pl.pallas_call(gather_kernel, out_shape=jax.ShapeDtypeStruct((2, BLOCKS,...]
  transfers between devices with their start and end apart: 4 -> 4, of which waited for: 2 -> 2; matrix products, arithmetic and copies ran while one was open for 5% -> 6% of each run, Pallas kernels for 47% -> 42%
where the time goes in v1:
time: 353 us; the launch traced here: 352 us
  Pallas kernels  285 us (81%)
  starting transfers between devices  23.8 us (7%)
  other arithmetic  21.5 us (6%)
  waiting for transfers between devices  7.93 us (2%)
  matrix products  7.07 us (2%)
  local copies, waits for them, and re-layouts  5.6 us (2%)
    pallas_call x1, Pallas kernels, return_call(): pl.pallas_call(return_kernel, out_shape=jax.ShapeDtypeStruct((rows, model...  148 us
    pallas_call x1, Pallas kernels, gather_call(): pl.pallas_call(gather_kernel, out_shape=jax.ShapeDtypeStruct((2, BLOCKS,...  137 us
    all_to_all x1, starting transfers between devices, gathered_shards(): lax.all_to_all(reply, both, split_axis=0, concat_axis=0, tiled=True)  13.2 us
    convert_element_type x1, other arithmetic, gathered_shards(): grad_second = (scaled * gate_act).astype(jnp.bfloat16)  7.33 us
  transfers between devices with their start and end apart: 4, of which 2 were waited for; matrix products, arithmetic and copies ran while one was open for 6% of the time, Pallas kernels for 42%

profile of v1, /device:TPU:8, one launch (start us, length us, event | category | flops | bytes accessed | tf_op | source)
XLA Modules:
  0.0 352.1 jit_solution(5304407168363236757)
XLA Ops:
  0.6 0.0 copy-start
  0.7 0.7 convert_reduce_fusion
  1.4 0.2 copy-done
  1.6 1.7 fusion.34
  3.3 0.0 copy-start.3
  3.3 0.0 copy-start.5
  3.4 0.0 copy-start.4
  3.4 0.2 fusion.11
  3.6 0.3 copy-done.3
  3.9 0.0 copy-done.5
  3.9 0.0 copy-done.4
  3.9 0.6 copy.43
  4.6 6.0 %all-to-all-start = ((f32[32,2,128]{2,1,0:T(2,128)}), f32[32,2,128]{2,1,0:T(2,128)S(1)}, u32[]{:S(2)}, u32[]{:S(2)}) async-start(f32[32,2,128]{2,1,0:T(2,128)} %copy.43), calls=%async_computation | async-start | bytes 65536 | tf_op jit(solution)/shard_map/all_to_all | solution.py:691
  11.3 2.3 copy.52
  13.5 0.5 and_select_fusion
  14.0 2.6 all-to-all-done
  16.7 0.3 fusion.33
  17.0 0.1 reshape.67
  17.1 0.1 broadcast_in_dim_tile.3
  17.2 1.0 fusion.16.place_ref
  18.1 0.0 copy-start.1
  18.1 136.8 %gather_upstream.1 = f32[2,16,64,768]{3,2,1,0:T(8,128)} custom-call(bf16[128,4096]{1,0:T(8,128)(2,1)} %bitcast.106, bf16[2,16,64,128]{3,2,1,0:T(8,128)(2,1)} %fusion.16.place_ref, bf16[768,4096]{1,0:T(8,128)(2,1)} %bitcast.101), custom_call_target="tpu_custom_call" | custom-call | tf_op jit(solution)/shard_map/gather_upstream/pallas_call | solution.py:394
  155.0 0.0 copy-done.1
  155.0 4.9 %fusion.8 = bf16[2,16,64]{2,1,0:T(8,128)(2,1)S(1)} fusion(f32[2,16,64,768]{3,2,1,0:T(8,128)} %gather_upstream.1, bf16[16,2,64,768]{3,2,1,0:T(8,128)(2,1)S(1)} %bitcast.97, bf16[16,2,64,768]{3,2,1,0:T(8,128)(2,1)} %bitcast.99), kind=kLoop, calls=%fused_computation.13 | loop fusion | flops 14153728 | bytes 12587008 | tf_op jit(solution)/shard_map/reduce_sum | solution.py:725
  159.8 0.7 select_reduce_fusion.1
  160.6 0.1 stack_broadcast_in_dim.2
  160.7 0.6 copy.49
  161.3 13.2 %all-to-all-start.1 = ((f32[32,2,128]{2,1,0:T(2,128)}), f32[32,2,128]{2,1,0:T(2,128)S(1)}, u32[]{:S(2)}, u32[]{:S(2)}) async-start(f32[32,2,128]{2,1,0:T(2,128)} %copy.49), calls=%async_computation.1 | async-start | bytes 65536 | tf_op jit(solution)/shard_map/all_to_all | solution.py:735
  174.6 0.6 constant_dynamic-slice_fusion.1
  175.2 0.1 collective-permute-start
  175.3 5.3 %all-to-all-done.1 = f32[32,2,128]{2,1,0:T(2,128)S(1)} async-done(((f32[32,2,128]{2,1,0:T(2,128)}), f32[32,2,128]{2,1,0:T(2,128)S(1)}, u32[]{:S(2)}, u32[]{:S(2)}) %all-to-all-start.1) | async-done | bytes 32800 | tf_op jit(solution)/shard_map/all_to_all | solution.py:735
  180.6 0.6 multiply_reduce_fusion.1
  181.2 0.3 fusion.23
  181.6 0.8 multiply_reduce_fusion
  182.3 0.8 multiply_convert_fusion.1
  183.1 2.5 convolution_bitcast_fusion
  185.6 4.4 %all-to-all-start.2 = ((f32[32,32,128]{2,1,0:T(8,128)}), f32[32,32,128]{2,1,0:T(8,128)}, u32[]{:S(2)}, u32[]{:S(2)}) async-start(f32[32,32,128]{2,1,0:T(8,128)} %convolution_bitcast_fusion), calls=%async_computation.2 | async-start | bytes 1048576 | tf_op jit(solution)/shard_map/all_to_all | solution.py:751
  190.0 0.0 copy-start.6
  190.0 7.3 %multiply_convert_fusion = (bf16[2,16,64,768]{3,2,1,0:T(8,128)(2,1)}, bf16[2,16,64,768]{3,2,1,0:T(8,128)(2,1)}) fusion(f32[2,16,64,768]{3,2,1,0:T(8,128)} %gather_upstream.1, f32[2,16,64]{2,1,0:T(8,128)S(1)} %copy.44, bf16[16,2,64,768]{3,2,1,0:T(8,128)(2,1)S(1)} %bitcast.98, bf16[16,2,64,768]{3,2,1,0:T(8,128)(2,1)} %bitcast.100), kind=kLoop, calls=%fused_computation.14 | loop fusion | flops 25165824 | bytes 18882560 | tf_op jit(solution)/shard_map/convert_element_type | solution.py:728
  197.3 0.0 collective-permute-done
  197.3 0.3 broadcast_in_dim.75
  197.7 0.3 broadcast_in_dim.74
  198.0 0.0 copy-done.6
  198.0 1.2 fusion.15.join_ref
  199.2 0.0 copy-start.2
  199.2 147.9 %back_return.1 = bf16[128,4096]{1,0:T(8,128)(2,1)} custom-call(bf16[2,16,64,768]{3,2,1,0:T(8,128)(2,1)} %get-tuple-element.8.first_ref, bf16[2,16,64,768]{3,2,1,0:T(8,128)(2,1)} %get-tuple-element.7.second_ref, bf16[16,128,128]{2,1,0:T(8,128)(2,1)} %fusion.15.join_ref, bf16[4096,768]{1,0:T(8,128)(2,1)} %bitcast.102, bf16[4096,768]{1,0:T(8,128)(2,1)} %bitcast.103), custom_call_target="tpu_custom_call" | custom-call | tf_op jit(solution)/shard_map/back_return/pallas_call | solution.py:627
  347.1 0.0 copy-done.2
  347.2 0.6 select_reduce_fusion.2
  347.8 2.6 fusion.10
  350.4 0.0 all-to-all-done.2
  350.4 1.7 reduce_sum.119
  (13 shorter events, 0.1 us)
Async XLA Ops:
  0.6 1.0 copy-start
  3.3 0.6 copy-start.3
  3.3 0.6 copy-start.5
  3.4 0.5 copy-start.4
  4.6 12.1 %all-to-all-start = ((f32[32,2,128]{2,1,0:T(2,128)}), f32[32,2,128]{2,1,0:T(2,128)S(1)}, u32[]{:S(2)}, u32[]{:S(2)}) async-start(f32[32,2,128]{2,1,0:T(2,128)} %copy.43), calls=%async_computation | async-start | bytes 65536 | tf_op jit(solution)/shard_map/all_to_all | solution.py:691
  18.1 136.8 %copy-start.1 = (bf16[1,2048,768]{2,1,0:T(8,128)(2,1)S(1)}, bf16[1,2048,768]{2,1,0:T(8,128)(2,1)}, u32[]{:S(2)}) copy-start(bf16[1,2048,768]{2,1,0:T(8,128)(2,1)} %param.16) | copy-start | bytes 9437188
  161.3 19.3 %all-to-all-start.1 = ((f32[32,2,128]{2,1,0:T(2,128)}), f32[32,2,128]{2,1,0:T(2,128)S(1)}, u32[]{:S(2)}, u32[]{:S(2)}) async-start(f32[32,2,128]{2,1,0:T(2,128)} %copy.49), calls=%async_computation.1 | async-start | bytes 65536 | tf_op jit(solution)/shard_map/all_to_all | solution.py:735
  175.2 22.2 %collective-permute-start = (f32[16,128]{1,0:T(8,128)}, f32[16,128]{1,0:T(8,128)S(1)}, u32[]{:S(2)}, u32[]{:S(2)}) collective-permute-start(f32[16,128]{1,0:T(8,128)} %bitcast.21), channel_id=1, source_target_pairs={{0,1},{1,0},{2,3},{3,2},{4,5},{5,4},{6,7},{7,6},{8,9},{9,8},{10,11... | collective-permute-start | bytes 24584 | tf_op jit(solution)/shard_map/ppermute | solution.py:708
  185.6 164.8 %all-to-all-start.2 = ((f32[32,32,128]{2,1,0:T(8,128)}), f32[32,32,128]{2,1,0:T(8,128)}, u32[]{:S(2)}, u32[]{:S(2)}) async-start(f32[32,32,128]{2,1,0:T(8,128)} %convolution_bitcast_fusion), calls=%async_computation.2 | async-start | bytes 1048576 | tf_op jit(solution)/shard_map/all_to_all | solution.py:751
  190.0 8.0 %copy-start.6 = (s32[128]{0:T(128)S(1)}, s32[128]{0:T(128)}, u32[]{:S(2)}) copy-start(s32[128]{0:T(128)} %and_select_fusion) | copy-start | bytes 1540
  199.2 148.0 %copy-start.2 = (s32[1,128,8]{1,2,0:T(8,128)S(1)}, s32[1,128,8]{1,2,0:T(8,128)}, u32[]{:S(2)}) copy-start(s32[1,128,8]{1,2,0:T(8,128)} %param.18) | copy-start | bytes 12292

commit v2 on v1

--- a/solution.py
+++ b/solution.py
@@ -166,6 +166,8 @@
 
 CHUNKS = len(GATHER_TYPES)
 LEVELS = 4
+AHEAD = 3
+PARTS = 4
 BLOCKS = 4 * LEVELS
 
 
@@ -235,13 +237,170 @@
     return [(code // 20, names(code // 20)[code % 20]) for code in order]
 
 
+def route(token_ref, router_ref, id_ref, probs_ref, gate_ref, letter):
+    experts, rows = probs_ref.shape
+    logits = lax.dot_general(
+        router_ref[...], token_ref[...], (((1,), (1,)), ((), ())), preferred_element_type=jnp.float32
+    )
+    shifted = jnp.exp(logits - jnp.max(logits, axis=0, keepdims=True))
+    probs = shifted / jnp.sum(shifted, axis=0, keepdims=True)
+    expert = lax.broadcasted_iota(jnp.int32, (experts, rows), 0)
+    picked = jnp.zeros((experts, rows), jnp.float32)
+    for k in range(id_ref.shape[0]):
+        picked = picked + (id_ref[k : k + 1, :] == expert).astype(jnp.float32)
+    chosen = probs * picked
+    gates = chosen / jnp.sum(chosen, axis=0, keepdims=True)
+    earlier = lax.broadcasted_iota(jnp.int32, (rows, rows), 0)
+    earlier = (earlier < lax.broadcasted_iota(jnp.int32, (rows, rows), 1)).astype(jnp.float32)
+    rank = jnp.dot(
+        picked.astype(jnp.bfloat16),
+        earlier.astype(jnp.bfloat16),
+        preferred_element_type=jnp.float32,
+    )
+    slot_pos = jnp.where(picked > 0, rank, -1.0)
+    sent_gates = gates.astype(jnp.bfloat16).astype(jnp.float32)
+    probs_ref[...] = probs
+    gate_ref[...] = gates
+    for e in range(experts):
+        letter[e, 0:1, :] = slot_pos[e : e + 1, :]
+        letter[e, 1:2, :] = sent_gates[e : e + 1, :]
+        letter[e, 2:3, :] = slot_pos[e ^ 1 : (e ^ 1) + 1, :]
+
+
+class Mail:
+    def __init__(self, outbox, inbox, send, recv):
+        z, x, y, c = place_of()
+        self.me = (z * 2 + x) * 4 + y * 2 + c
+        self.outbox, self.inbox, self.send, self.recv = outbox, inbox, send, recv
+        self.devices = outbox.shape[0]
+
+    def copies(self):
+        for step in range(1, self.devices):
+            to = (self.me + step) % self.devices
+            yield pltpu.make_async_remote_copy(
+                src_ref=self.outbox.at[to],
+                dst_ref=self.inbox.at[self.me],
+                send_sem=self.send.at[step],
+                recv_sem=self.recv.at[step],
+                device_id=(to // 4, to % 4),
+                device_id_type=MESH,
+            )
+
+    def post(self):
+        self.inbox[self.me] = self.outbox[self.me]
+        for copy in self.copies():
+            copy.start()
+
+    def collect(self):
+        for step in range(1, self.devices):
+            ref = self.inbox.at[(self.me - step + self.devices) % self.devices]
+            pltpu.make_async_remote_copy(
+                src_ref=ref,
+                dst_ref=ref,
+                send_sem=self.send.at[step],
+                recv_sem=self.recv.at[step],
+                device_id=(self.me // 4, self.me % 4),
+                device_id_type=MESH,
+            ).wait_recv()
+
+    def close(self):
+        for copy in self.copies():
+            copy.wait_send()
+
+
 def gather_kernel(
-    grad_ref, place_ref, down_ref, up_ref, held, rows, down, own_sem, down_sem, send, recv, peer_send, peer_recv
+    grad_ref,
+    down_ref,
+    token_ref,
+    router_ref,
+    id_ref,
+    pre_gate_ref,
+    pre_up_ref,
+    first_ref,
+    second_ref,
+    met_ref,
+    reply,
+    probs_ref,
+    gate_ref,
+    held,
+    up_ref,
+    rows,
+    down,
+    saved,
+    grads,
+    letter,
+    inbox,
+    own_sem,
+    down_sem,
+    saved_sem,
+    grads_sem,
+    send,
+    recv,
+    peer_send,
+    peer_recv,
+    mail_send,
+    mail_recv,
 ):
     z, x, y, c = place_of()
     width = held.shape[-1]
+    capacity = rows.shape[1]
+    tok_rows = held.shape[-2]
     here = (z * 2 + x) * 2 + y
     started = []
+    mail = Mail(letter, inbox, mail_send, mail_recv)
+
+    def spots(core, b):
+        slot = lax.broadcasted_iota(jnp.int32, (capacity, tok_rows), 0).astype(jnp.float32)
+        return inbox[b * 2 + core, 0:1, :] == slot
+
+    def saved_copies():
+        return [
+            pltpu.make_async_copy(ref, saved.at[i], saved_sem.at[i])
+            for i, ref in enumerate((pre_gate_ref, pre_up_ref))
+        ]
+
+    def grad_copies(core, turn):
+        return [
+            pltpu.make_async_copy(grads.at[i, core], ref.at[core], grads_sem.at[turn, i])
+            for i, ref in enumerate((first_ref, second_ref))
+        ]
+
+    def count():
+        sources = inbox.shape[0]
+        taken = (inbox[:, 0, :] >= 0).astype(jnp.bfloat16)
+        one = lax.broadcasted_iota(jnp.int32, (sources, sources), 0) % 4
+        two = lax.broadcasted_iota(jnp.int32, (sources, sources), 1) % 4
+        alike = (one == two).astype(jnp.float32).astype(jnp.bfloat16)
+        total = jnp.dot(alike, taken, preferred_element_type=jnp.float32)
+        total = jnp.broadcast_to(jnp.sum(total, axis=1, keepdims=True), total.shape)
+        for s in range(sources):
+            reply[s, 1:2, :] = total[s : s + 1, :]
+
+    def prepare(part):
+        @pl.loop(part * BLOCKS // PARTS, (part + 1) * BLOCKS // PARTS)
+        def _(b):
+            for core in range(2):
+                first = saved[0, b * 2 + core].astype(jnp.float32)
+                second = saved[1, b * 2 + core].astype(jnp.float32)
+                sig = jax.nn.sigmoid(first)
+                grads[0, core, b] = (second * sig * (1.0 + first * (1.0 - sig))).astype(jnp.bfloat16)
+                grads[1, core, b] = (first * sig).astype(jnp.bfloat16)
+
+    def finish(core):
+        @pl.loop(0, BLOCKS)
+        def _(b):
+            source = b * 2 + core
+            upstream = up_ref[core, b]
+            act = grads[1, core, b].astype(jnp.float32)
+            at = spots(core, b)
+            gate = jnp.sum(jnp.where(at, inbox[source, 1:2, :], 0.0), axis=1, keepdims=True)
+            hidden = act * saved[1, source].astype(jnp.float32)
+            combine = jnp.sum(upstream * hidden, axis=1, keepdims=True)
+            combine = combine.astype(jnp.bfloat16).astype(jnp.float32)
+            reply[source, 0:1, :] = jnp.sum(jnp.where(at, combine, 0.0), axis=0, keepdims=True)
+            scaled = gate * upstream
+            grads[0, core, b] = (scaled * grads[0, core, b].astype(jnp.float32)).astype(jnp.bfloat16)
+            grads[1, core, b] = (scaled * act).astype(jnp.bfloat16)
 
     def start(copy, when=None):
         if when is None:
@@ -264,7 +423,9 @@
         @pl.loop(0, BLOCKS, unroll=4)
         def _(b):
             rows[b] = jnp.dot(
-                place_ref[core, b], held[chunk, core, b], preferred_element_type=jnp.float32
+                spots(core, b).astype(jnp.float32).astype(jnp.bfloat16),
+                held[chunk, core, b],
+                preferred_element_type=jnp.float32,
             ).astype(jnp.bfloat16)
 
         group = 4
@@ -376,46 +537,103 @@
         own_copy(chunk).start()
     down_copy(0).start()
     down_copy(1).start()
-    for chunk, name in listed(GATHER_ORDER, gather_names):
+    for copy in saved_copies():
+        copy.start()
+    steps = listed(GATHER_ORDER, gather_names)
+    ahead = [s for s in steps if s[1][0] == "own"][:AHEAD]
+    for chunk, name in ahead:
         step(chunk, name)
+    route(token_ref, router_ref, id_ref, probs_ref, gate_ref, letter)
+    mail.post()
+    met, part = False, 0
+    for at, (chunk, name) in enumerate(steps):
+        if (chunk, name) in ahead:
+            continue
+        if at % 5 == 0 and at > 10 and part < PARTS:
+            if part == 0:
+                for copy in saved_copies():
+                    copy.wait()
+            prepare(part)
+            part += 1
+        if name[0] == "near" and not met:
+            mail.collect()
+            count()
+            met = True
+        step(chunk, name)
+    for turn, core in enumerate((c, 1 - c)):
+        finish(core)
+        for copy in grad_copies(core, turn):
+            copy.start()
+    met_ref[...] = inbox[...]
     for copy, when in started:
         if when is None:
             copy.wait_send()
         else:
             pl.when(when)(copy.wait_send)
-
-
-def gather_call(grad, place, down_weight):
+    mail.close()
+    for turn, core in enumerate((c, 1 - c)):
+        for copy in grad_copies(core, turn):
+            copy.wait()
+
+
+def gather_call(grad, down_weight, tokens, router, ids, pre_gate, pre_up):
     rows, model_width = grad.shape
     hidden = down_weight.shape[0]
-    capacity = place.shape[2]
+    devices = 2 * BLOCKS
+    capacity = pre_gate.shape[0] // devices
+    experts = router.shape[0]
     width = model_width // CHUNKS
     dma = pltpu.SemaphoreType.DMA
+    vmem, anywhere = pl.BlockSpec(memory_space=pltpu.VMEM), pl.BlockSpec(memory_space=pl.ANY)
+    halves = (2, BLOCKS, capacity, hidden)
+    small = (devices, 8, rows)
+    post = pltpu.VMEM(small, jnp.float32)
+    blocked = (devices, capacity, hidden)
     return pl.pallas_call(
         gather_kernel,
-        out_shape=jax.ShapeDtypeStruct((2, BLOCKS, capacity, hidden), jnp.float32),
-        in_specs=[
-            pl.BlockSpec(memory_space=pl.ANY),
-            pl.BlockSpec(memory_space=pltpu.VMEM),
-            pl.BlockSpec(memory_space=pl.ANY),
-        ],
-        out_specs=pl.BlockSpec(memory_space=pltpu.VMEM),
+        out_shape=(
+            jax.ShapeDtypeStruct(halves, jnp.bfloat16),
+            jax.ShapeDtypeStruct(halves, jnp.bfloat16),
+            jax.ShapeDtypeStruct(small, jnp.float32),
+            jax.ShapeDtypeStruct(small, jnp.float32),
+            jax.ShapeDtypeStruct((experts, rows), jnp.float32),
+            jax.ShapeDtypeStruct((experts, rows), jnp.float32),
+        ),
+        in_specs=[anywhere, anywhere, vmem, vmem, vmem, anywhere, anywhere],
+        out_specs=(anywhere, anywhere, vmem, vmem, vmem, vmem),
         scratch_shapes=[
             pltpu.VMEM((CHUNKS, 2, BLOCKS, rows, width), jnp.bfloat16),
+            pltpu.VMEM(halves, jnp.float32),
             pltpu.VMEM((BLOCKS, capacity, width), jnp.bfloat16),
             pltpu.VMEM((2, hidden, width), jnp.bfloat16),
+            pltpu.VMEM((2, *blocked), jnp.bfloat16),
+            pltpu.VMEM((2, *halves), jnp.bfloat16),
+            post,
+            post,
             dma((CHUNKS,)),
             dma((CHUNKS,)),
+            dma((2,)),
+            dma((2, 2)),
             dma((CHUNKS, 19)),
             dma((CHUNKS, BLOCKS)),
             dma((CHUNKS,)),
             dma((CHUNKS,)),
+            dma((devices,)),
+            dma((devices,)),
         ],
         compiler_params=pltpu.CompilerParams(
-            has_side_effects=True, vmem_limit_bytes=60 * 2**20
+            has_side_effects=True, vmem_limit_bytes=62 * 2**20
         ),
         name="gather_upstream",
-    )(grad, place, down_weight)
+    )(
+        grad,
+        down_weight,
+        tokens,
+        router,
+        ids,
+        pre_gate.reshape(blocked),
+        pre_up.reshape(blocked),
+    )
 
 
 def return_names(chunk):
@@ -433,7 +651,16 @@
     join_ref,
     gate_ref,
     up_ref,
+    reply,
+    probs_ref,
+    share_ref,
+    id_ref,
+    aux_ref,
+    token_ref,
+    router_ref,
     out_ref,
+    combine_ref,
+    total_ref,
     held,
     landed,
     leaving,
@@ -443,8 +670,47 @@
     recv,
     peer_send,
     peer_recv,
+    answers,
+    slope,
+    outbox,
+    inbox,
+    reply_send,
+    reply_recv,
+    mail_send,
+    mail_recv,
 ):
     z, x, y, c = place_of()
+    replies = Mail(reply, answers, reply_send, reply_recv)
+    mail = Mail(outbox, inbox, mail_send, mail_recv)
+    tok_rows = token_ref.shape[0]
+    experts = router_ref.shape[0]
+
+    def route_back():
+        probs, gates = probs_ref[...], share_ref[...]
+        expert = lax.broadcasted_iota(jnp.int32, (experts, tok_rows), 0)
+        picked = jnp.zeros((experts, tok_rows), jnp.float32)
+        for k in range(id_ref.shape[0]):
+            picked = picked + (id_ref[k : k + 1, :] == expert).astype(jnp.float32)
+        chosen_sum = jnp.sum(probs * picked, axis=0, keepdims=True)
+        combine = answers[:, 0, :]
+        combine_ref[...] = combine
+        mixed = jnp.sum(gates * combine, axis=0, keepdims=True)
+        prob_grad = picked * (combine - mixed) / chosen_sum
+        pairs = id_ref.shape[0] * tok_rows * 2 * LEVELS
+        prob_grad = prob_grad + aux_ref[0] * (experts * answers[:, 1, :] / pairs)
+        mean = jnp.sum(probs * prob_grad, axis=0, keepdims=True)
+        logit_grad = probs * (prob_grad - mean)
+        slope[...] = jnp.transpose(logit_grad).astype(jnp.bfloat16)
+        part = token_ref.shape[1] // outbox.shape[0]
+
+        @pl.loop(0, outbox.shape[0])
+        def _(d):
+            outbox[d] = jnp.dot(
+                logit_grad.astype(jnp.bfloat16),
+                token_ref[:, pl.ds(pl.multiple_of(d * part, part), part)],
+                preferred_element_type=jnp.float32,
+            ).astype(jnp.bfloat16)
+
     capacity = first_ref.shape[2]
     width = held.shape[-1]
     hidden = first_ref.shape[3]
@@ -601,13 +867,26 @@
             else:
                 take_ends(block, 8)
                 take(block, 18)
-            out_ref[:, chunk * width : (chunk + 1) * width] = held[chunk, block]
+            here = slice(chunk * width, (chunk + 1) * width)
+            routed = jnp.dot(slope[...], router_ref[:, here], preferred_element_type=jnp.float32)
+            out_ref[:, here] = (held[chunk, block].astype(jnp.float32) + routed).astype(jnp.bfloat16)
 
     for chunk in range(2):
         for copy in weight_copies(chunk):
             copy.start()
+    replies.post()
+    begun = False
     for chunk, name in listed(RETURN_ORDER, return_names):
         step(chunk, name)
+        if not begun:
+            begun = True
+            replies.collect()
+            route_back()
+            mail.post()
+    mail.collect()
+    total_ref[...] = jnp.sum(inbox[...].astype(jnp.float32), axis=0)
+    replies.close()
+    mail.close()
     for chunk in range(CHUNKS - 2, CHUNKS):
         leave(chunk).wait_send()
     for copy, when in started:
@@ -617,18 +896,28 @@
             pl.when(when)(copy.wait_send)
 
 
-def return_call(first, second, joined, gate_weight, up_weight):
+def return_call(
+    first, second, joined, gate_weight, up_weight, reply, probs, shares, ids, aux, tokens, router
+):
     model_width, hidden = gate_weight.shape
     capacity = first.shape[2]
     rows = joined.shape[1]
+    experts, devices = router.shape[0], reply.shape[0]
     width = model_width // CHUNKS
     dma = pltpu.SemaphoreType.DMA
     vmem, anywhere = pl.BlockSpec(memory_space=pltpu.VMEM), pl.BlockSpec(memory_space=pl.ANY)
+    post = pltpu.VMEM((devices, experts, model_width // devices), jnp.bfloat16)
     return pl.pallas_call(
         return_kernel,
-        out_shape=jax.ShapeDtypeStruct((rows, model_width), jnp.bfloat16),
-        in_specs=[vmem, vmem, vmem, anywhere, anywhere],
-        out_specs=vmem,
+        out_shape=(
+            jax.ShapeDtypeStruct((rows, model_width), jnp.bfloat16),
+            jax.ShapeDtypeStruct((experts, rows), jnp.float32),
+            jax.ShapeDtypeStruct((experts, model_width // devices), jnp.float32),
+        ),
+        in_specs=[vmem, vmem, vmem, anywhere, anywhere]
+        + [vmem] * 4
+        + [pl.BlockSpec(memory_space=pltpu.SMEM), vmem, vmem],
+        out_specs=(vmem, vmem, vmem),
         scratch_shapes=[
             pltpu.VMEM((CHUNKS, BLOCKS, rows, width), jnp.bfloat16),
             pltpu.VMEM((CHUNKS, 19, rows, width), jnp.bfloat16),
@@ -639,20 +928,20 @@
             dma((CHUNKS, 19)),
             dma((CHUNKS,)),
             dma((CHUNKS,)),
+            pltpu.VMEM(reply.shape, jnp.float32),
+            pltpu.VMEM((rows, experts), jnp.bfloat16),
+            post,
+            post,
+            dma((devices,)),
+            dma((devices,)),
+            dma((devices,)),
+            dma((devices,)),
         ],
         compiler_params=pltpu.CompilerParams(
             has_side_effects=True, vmem_limit_bytes=60 * 2**20
         ),
         name="back_return",
-    )(first, second, joined, gate_weight, up_weight)
-
-
-def silu_terms(pre_gate, pre_up):
-    first = pre_gate.astype(jnp.float32)
-    second = pre_up.astype(jnp.float32)
-    gate_sig = jax.nn.sigmoid(first)
-    gate_act = first * gate_sig
-    return second * gate_sig * (1.0 + first * (1.0 - gate_sig)), gate_act, gate_act * second
+    )(first, second, joined, gate_weight, up_weight, reply, probs, shares, ids, aux, tokens, router)
 
 
 def gathered_shards(
@@ -667,96 +956,48 @@
     expert_ids,
     aux_weight,
 ):
-    both = ("seq", "exp")
-    seq_size = lax.axis_size("seq")
-    exp_size = lax.axis_size("exp")
-    devices = seq_size * exp_size
     inputs = tokens[0]
     chosen_ids = expert_ids[0]
-    tok_rows, top_count = chosen_ids.shape
-    model_width = inputs.shape[1]
+    tok_rows = chosen_ids.shape[0]
     experts = router_weight.shape[1]
+    devices = lax.axis_size("seq") * lax.axis_size("exp")
     capacity = saved_gate.shape[1] // devices
-
-    logits = jnp.dot(inputs, router_weight, preferred_element_type=jnp.float32)
-    router_probs = jax.nn.softmax(logits, axis=-1)
-    onehot = (chosen_ids[:, :, None] == jnp.arange(experts, dtype=jnp.int32)).astype(jnp.float32)
-    picked = jnp.sum(onehot, axis=1)
-    chosen_sum = jnp.sum(router_probs * picked, axis=1, keepdims=True)
-    gate_dense = router_probs * picked / chosen_sum
-    earlier = jnp.tril(jnp.ones((tok_rows, tok_rows), jnp.bfloat16), -1)
-    rank = jnp.dot(earlier, picked.astype(jnp.bfloat16), preferred_element_type=jnp.float32)
-    slot_pos = jnp.where(picked > 0, rank, -1.0)
-    sent = jnp.stack([slot_pos.T, gate_dense.astype(jnp.bfloat16).astype(jnp.float32).T], axis=1)
-    received = lax.all_to_all(sent, both, split_axis=0, concat_axis=0, tiled=True)
-
-    counts = jnp.sum((received[:, 0] >= 0).astype(jnp.float32), axis=1)
-    counts = jnp.tile(jnp.sum(counts.reshape(seq_size, exp_size), axis=0), seq_size)
-
-    def by_core(value):
-        return jnp.swapaxes(value.reshape((devices // 2, 2) + value.shape[1:]), 0, 1)
+    router, ids = router_weight.T, chosen_ids.T
+
+    grad_first, grad_second, met, reply, router_probs, gate_dense = gather_call(
+        out_grad[0], down_weight[0], inputs, router, ids, saved_gate[0], saved_up[0]
+    )
 
     here_core = lax.axis_index("exp") % 2
-    pos = received[:, 0].astype(jnp.int32)
-    slot_ids = jnp.arange(capacity, dtype=jnp.int32)[None, :, None]
-    at_slot = pos[:, None, :] == slot_ids
-    gate_rows = jnp.sum(jnp.where(at_slot, received[:, 1][:, None, :], 0.0), axis=2)[:, :, None]
-    place = by_core(at_slot.astype(jnp.bfloat16))
-    pos_by_core = by_core(received[:, 0])
-    own_pos = lax.dynamic_index_in_dim(pos_by_core, here_core, 0, keepdims=False)
-    sent_pos = lax.dynamic_index_in_dim(pos_by_core, 1 - here_core, 0, keepdims=False)
-    other_pos = lax.ppermute(sent_pos, "exp", [(i, i ^ 1) for i in range(exp_size)])
+    met = lax.dynamic_index_in_dim(
+        met.reshape((devices // 2, 2) + met.shape[1:]), here_core, 1, keepdims=False
+    )
     join_pos = jnp.concatenate(
         [
-            jnp.broadcast_to(own_pos[:, :, None], (devices // 2, tok_rows, capacity)),
-            jnp.broadcast_to(other_pos[:, :, None], (devices // 2, tok_rows, capacity)),
+            jnp.broadcast_to(met[:, i, :, None], (devices // 2, tok_rows, capacity))
+            for i in (0, 2)
         ],
         axis=2,
     ).astype(jnp.int32)
     joined = (join_pos == jnp.arange(2 * capacity, dtype=jnp.int32) % capacity).astype(jnp.bfloat16)
 
-    upstream = gather_call(out_grad[0], place, down_weight[0])
-
-    hidden_width = saved_gate.shape[2]
-    blocks = (devices, capacity, hidden_width)
-    slope, gate_act, hidden = silu_terms(
-        by_core(saved_gate[0].reshape(blocks)), by_core(saved_up[0].reshape(blocks))
-    )
-    slot_combine = jnp.sum(upstream * hidden, axis=-1).astype(jnp.bfloat16)
-    scaled = by_core(gate_rows) * upstream
-    grad_first = (scaled * slope).astype(jnp.bfloat16)
-    grad_second = (scaled * gate_act).astype(jnp.bfloat16)
-
-    slot_combine = jnp.swapaxes(slot_combine, 0, 1).reshape(devices, capacity)
-    combine_tok = jnp.sum(
-        jnp.where(at_slot, slot_combine.astype(jnp.float32)[:, :, None], 0.0), axis=1
-    )
-    reply = jnp.stack([combine_tok, jnp.broadcast_to(counts[:, None], combine_tok.shape)], axis=1)
-    answered = lax.all_to_all(reply, both, split_axis=0, concat_axis=0, tiled=True)
-
-    expert_sum = return_call(grad_first, grad_second, joined, gate_weight[0], up_weight[0])
-
-    combine_dense = answered[:, 0].T
-    seq_counts = answered[:, 1, 0]
-    combine_grad = jnp.sum(onehot * combine_dense[:, None, :], axis=2)
-    mixed = jnp.sum(gate_dense * combine_dense, axis=1, keepdims=True)
-    prob_grad = picked * (combine_dense - mixed) / chosen_sum
-    fraction = experts * seq_counts / (top_count * tok_rows * seq_size)
-    prob_grad = prob_grad + aux_weight[0] * fraction[None, :]
-    dlogits = router_probs * (prob_grad - jnp.sum(router_probs * prob_grad, axis=1, keepdims=True))
-    logit_grad = dlogits.astype(jnp.bfloat16)
-
-    router_terms = jnp.einsum("te,td->ed", logit_grad, inputs, preferred_element_type=jnp.float32)
-    router_terms = router_terms.reshape(experts, devices, model_width // devices)
-    router_terms = lax.all_to_all(
-        router_terms.transpose(1, 0, 2), both, split_axis=0, concat_axis=0, tiled=True
-    )
-    router_grad = jnp.sum(router_terms, axis=0).T
-
-    token_grad = expert_sum.astype(jnp.float32) + jnp.einsum(
-        "te,de->td", logit_grad, router_weight, preferred_element_type=jnp.float32
-    )
-    return (token_grad.astype(jnp.bfloat16)[None], combine_grad[None], router_grad)
+    token_grad, combine_dense, router_grad = return_call(
+        grad_first,
+        grad_second,
+        joined,
+        gate_weight[0],
+        up_weight[0],
+        reply,
+        router_probs,
+        gate_dense,
+        ids,
+        aux_weight,
+        inputs,
+        router,
+    )
+    onehot = chosen_ids[:, None, :] == jnp.arange(experts, dtype=jnp.int32)[:, None]
+    combine_grad = jnp.sum(jnp.where(onehot, combine_dense.T[:, :, None], 0.0), axis=1)
+    return (token_grad[None], combine_grad[None], router_grad.T)
 
 
 def program(*arrays):

time: 353 us -> 320 us (0.907)
  Pallas kernels: 285 us -> 310 us
  starting transfers between devices: 23.8 us -> 0 us
  other arithmetic: 21.5 us -> 2.52 us
  waiting for transfers between devices: 7.93 us -> 0 us
  matrix products: 7.07 us -> 0 us
    pallas_call x2, Pallas kernels: 285 us -> 310 us  [the longest x1 164 us: return_call(): pl.pallas_call(return_kernel, out_shape=(jax.ShapeDtypeStruct((rows, mode...]
    all_to_all x3 -> x0, starting transfers between devices: 23.7 us -> none  [the longest x1 13.2 us: gathered_shards(): lax.all_to_all(reply, both, split_axis=0, concat_axis=0, tiled=True)]
    convert_element_type x4 -> x0, other arithmetic: 9.04 us -> none  [the longest x1 7.33 us: gathered_shards(): grad_second = (scaled * gate_act).astype(jnp.bfloat16)]
    reduce_sum x10 -> x1, other arithmetic: 10.1 us -> 1.35 us  [gathered_shards(): jnp.sum(jnp.where(onehot, combine_dense.T[:, :, None], 0.0), axis=1)]
    all_to_all x3 -> x0, waiting for transfers between devices: 7.93 us -> none  [the longest x1 5.3 us: gathered_shards(): lax.all_to_all(reply, both, split_axis=0, concat_axis=0, tiled=True)]
    dot_general x4 -> x0, matrix products: 7.07 us -> none  [the longest x1 2.65 us: gathered_shards(): jnp.einsum('te,de->td', logit_grad, router_weight, preferred_element_type...]
  transfers between devices with their start and end apart: 4 -> 0, of which waited for: 2 -> 0; matrix products, arithmetic and copies ran while one was open for 6% -> 0% of each run, Pallas kernels for 42% -> 0%
where the time goes in v2:
time: 320 us; the launch traced here: 319 us
  Pallas kernels  310 us (97%)
  local copies, waits for them, and re-layouts  5.14 us (2%)
    pallas_call x1, Pallas kernels, return_call(): pl.pallas_call(return_kernel, out_shape=(jax.ShapeDtypeStruct((rows, mode...  164 us
    pallas_call x1, Pallas kernels, gather_call(): pl.pallas_call(gather_kernel, out_shape=(jax.ShapeDtypeStruct(halves, jnp...  147 us

profile of v2, /device:TPU:8, one launch (start us, length us, event | category | flops | bytes accessed | tf_op | source)
XLA Modules:
  0.0 319.2 jit_solution(773749020551702949)
XLA Ops:
  0.6 146.5 %gather_upstream.1 = (bf16[2,16,64,768]{3,2,1,0:T(8,128)(2,1)}, bf16[2,16,64,768]{3,2,1,0:T(8,128)(2,1)}, f32[32,8,128]{2,1,0:T(8,128)}, f32[32,8,128]{2,1,0:T(8...) custom-call(bf16[128,4096]{1,0:T(8,128)(2,1)} %bitcast.32, bf16[768,4096]{1,0:T(8,128)(2,1)} %bitcast.23, ...), custom_call_target="tpu_custom_call" | custom-call | tf_op jit(solution)/shard_map/gather_upstream/pallas_call | solution.py:592
  147.2 0.9 constant_dynamic-slice_fusion
  148.1 0.3 broadcast_in_dim.35
  148.4 0.3 broadcast_in_dim.37
  148.8 1.2 fusion.1.join_ref
  150.6 0.0 copy-start
  150.6 163.7 %back_return.1 = (bf16[128,4096]{1,0:T(8,128)(2,1)}, f32[32,128]{1,0:T(8,128)}, f32[32,128]{1,0:T(8,128)}) custom-call(bf16[2,16,64,768]{3,2,1,0:T(8,128)(2,1)} %get-tuple-element.12.first_ref, bf16[2,16,64,768]{3,2,1,0:T(8,128)(2,1)} %get-tuple-element.13.second_ref, bf16[16,128,128]{2,1,0:T(8,128)(2,1)} %fusion.1.join_ref, bf16[4096,768]{1,0:T(8,128)(2,1)} %bitcast.24, ...), custom_call_target="tpu_custom_call" | custom-call | tf_op jit(solution)/shard_map/back_return/pallas_call | solution.py:910
  314.3 0.0 copy-done
  314.3 1.3 select_reduce_fusion
  315.6 2.3 copy.22
  317.9 1.3 copy.23
  (3 shorter events, 0.0 us)
Async XLA Ops:
  150.6 163.7 %copy-start = (s32[1,128,8]{1,2,0:T(8,128)S(1)}, s32[1,128,8]{1,2,0:T(8,128)}, u32[]{:S(2)}) copy-start(s32[1,128,8]{1,2,0:T(8,128)} %param.18) | copy-start | bytes 12292

commit v3 on v2

--- a/solution.py
+++ b/solution.py
@@ -318,7 +318,7 @@
     pre_up_ref,
     first_ref,
     second_ref,
-    met_ref,
+    join_ref,
     reply,
     probs_ref,
     gate_ref,
@@ -376,6 +376,16 @@
         for s in range(sources):
             reply[s, 1:2, :] = total[s : s + 1, :]
 
+    def join():
+        slot = lax.broadcasted_iota(jnp.int32, (capacity, tok_rows), 0).astype(jnp.float32)
+
+        @pl.loop(0, BLOCKS)
+        def _(b):
+            both = [
+                (inbox[b * 2 + c, row : row + 1, :] == slot).astype(jnp.float32) for row in (0, 2)
+            ]
+            join_ref[b] = jnp.transpose(jnp.concatenate(both, axis=0)).astype(jnp.bfloat16)
+
     def prepare(part):
         @pl.loop(part * BLOCKS // PARTS, (part + 1) * BLOCKS // PARTS)
         def _(b):
@@ -408,6 +418,11 @@
         else:
             pl.when(when)(copy.start)
         started.append((copy, when))
+
+    def over(chunk, core, turn):
+        level = nearest(z, turn)
+        ref = held.at[chunk, core, pl.ds(level * 4, 4)]
+        return sibling_copy(ref, ref, peer_send.at[chunk, turn], peer_recv.at[chunk, turn])
 
     def own_copy(chunk):
         return pltpu.make_async_copy(
@@ -518,17 +533,16 @@
             onward(block, level, 7 + k)
             spread(block, 15 + k, dq=1)
         elif kind == "Q":
-            for other in range(LEVELS):
+            for turn in range(LEVELS):
                 for side in range(2):
-                    arrived(near.block(other, side, 1 - q))
-            ref = held.at[chunk, c]
-            start(sibling_copy(ref, ref, peer_send.at[chunk], peer_recv.at[chunk]))
+                    arrived(near.block(nearest(z, turn), side, 1 - q))
+                start(over(chunk, c, turn))
         elif kind == "near":
             down_copy(chunk).wait()
             multiply(chunk, c)
         elif kind == "far":
-            ref = held.at[chunk, 1 - c]
-            sibling_copy(ref, ref, peer_send.at[chunk], peer_recv.at[chunk]).wait_recv()
+            for turn in range(LEVELS):
+                over(chunk, 1 - c, turn).wait_recv()
             multiply(chunk, 1 - c)
             if chunk + 2 < CHUNKS:
                 down_copy(chunk + 2).start()
@@ -558,13 +572,13 @@
         if name[0] == "near" and not met:
             mail.collect()
             count()
+            join()
             met = True
         step(chunk, name)
     for turn, core in enumerate((c, 1 - c)):
         finish(core)
         for copy in grad_copies(core, turn):
             copy.start()
-    met_ref[...] = inbox[...]
     for copy, when in started:
         if when is None:
             copy.wait_send()
@@ -594,7 +608,7 @@
         out_shape=(
             jax.ShapeDtypeStruct(halves, jnp.bfloat16),
             jax.ShapeDtypeStruct(halves, jnp.bfloat16),
-            jax.ShapeDtypeStruct(small, jnp.float32),
+            jax.ShapeDtypeStruct((BLOCKS, rows, 2 * capacity), jnp.bfloat16),
             jax.ShapeDtypeStruct(small, jnp.float32),
             jax.ShapeDtypeStruct((experts, rows), jnp.float32),
             jax.ShapeDtypeStruct((experts, rows), jnp.float32),
@@ -616,8 +630,8 @@
             dma((2, 2)),
             dma((CHUNKS, 19)),
             dma((CHUNKS, BLOCKS)),
-            dma((CHUNKS,)),
-            dma((CHUNKS,)),
+            dma((CHUNKS, LEVELS)),
+            dma((CHUNKS, LEVELS)),
             dma((devices,)),
             dma((devices,)),
         ],
@@ -958,29 +972,12 @@
 ):
     inputs = tokens[0]
     chosen_ids = expert_ids[0]
-    tok_rows = chosen_ids.shape[0]
     experts = router_weight.shape[1]
-    devices = lax.axis_size("seq") * lax.axis_size("exp")
-    capacity = saved_gate.shape[1] // devices
     router, ids = router_weight.T, chosen_ids.T
 
-    grad_first, grad_second, met, reply, router_probs, gate_dense = gather_call(
+    grad_first, grad_second, joined, reply, router_probs, gate_dense = gather_call(
         out_grad[0], down_weight[0], inputs, router, ids, saved_gate[0], saved_up[0]
     )
-
-    here_core = lax.axis_index("exp") % 2
-    met = lax.dynamic_index_in_dim(
-        met.reshape((devices // 2, 2) + met.shape[1:]), here_core, 1, keepdims=False
-    )
-    join_pos = jnp.concatenate(
-        [
-            jnp.broadcast_to(met[:, i, :, None], (devices // 2, tok_rows, capacity))
-            for i in (0, 2)
-        ],
-        axis=2,
-    ).astype(jnp.int32)
-    joined = (join_pos == jnp.arange(2 * capacity, dtype=jnp.int32) % capacity).astype(jnp.bfloat16)
-
     token_grad, combine_dense, router_grad = return_call(
         grad_first,
         grad_second,

time: 320 us -> 317 us (level)
  no operation moved by 1% of the time
where the time goes in v3:
time: 317 us
  Pallas kernels  311 us (98%)
  local copies, waits for them, and re-layouts  3.62 us (1%)
    pallas_call x1, Pallas kernels, return_call(): pl.pallas_call(return_kernel, out_shape=(jax.ShapeDtypeStruct((rows, mode...  164 us
    pallas_call x1, Pallas kernels, gather_call(): pl.pallas_call(gather_kernel, out_shape=(jax.ShapeDtypeStruct(halves, jnp...  147 us

profile of v3, /device:TPU:8, one launch (start us, length us, event | category | flops | bytes accessed | tf_op | source)
XLA Modules:
  0.0 317.1 jit_solution(6512286574180228581)
XLA Ops:
  1.3 147.1 %gather_upstream.1 = (bf16[2,16,64,768]{3,2,1,0:T(8,128)(2,1)}, bf16[2,16,64,768]{3,2,1,0:T(8,128)(2,1)}, bf16[16,128,128]{2,1,0:T(8,128)(2,1)}, f32[32,8,128]{2...) custom-call(bf16[128,4096]{1,0:T(8,128)(2,1)} %bitcast.24, bf16[768,4096]{1,0:T(8,128)(2,1)} %bitcast.15, ...), custom_call_target="tpu_custom_call" | custom-call | tf_op jit(solution)/shard_map/gather_upstream/pallas_call | solution.py:606
  148.4 0.0 copy-start
  148.4 163.7 %back_return.1 = (bf16[128,4096]{1,0:T(8,128)(2,1)}, f32[32,128]{1,0:T(8,128)}, f32[32,128]{1,0:T(8,128)}) custom-call(bf16[2,16,64,768]{3,2,1,0:T(8,128)(2,1)} %get-tuple-element.12.first_ref, bf16[2,16,64,768]{3,2,1,0:T(8,128)(2,1)} %get-tuple-element.13.second_ref, bf16[16,128,128]{2,1,0:T(8,128)(2,1)} %get-tuple-element.14.join_ref, ...), custom_call_target="tpu_custom_call" | custom-call | tf_op jit(solution)/shard_map/back_return/pallas_call | solution.py:924
  312.1 0.0 copy-done
  312.2 1.3 select_reduce_fusion
  313.5 2.3 copy.18
  315.8 1.3 copy.19
Async XLA Ops:
  148.4 163.7 %copy-start = (s32[1,128,8]{1,2,0:T(8,128)S(1)}, s32[1,128,8]{1,2,0:T(8,128)}, u32[]{:S(2)}) copy-start(s32[1,128,8]{1,2,0:T(8,128)} %param.18) | copy-start | bytes 12292
